TPU v7x, 32 devices: a whole 2x2x4 slice. The times are simulated.
32 devices in a mesh: robot: 8 (over z, x), sub: 4 (over y, core).
Axes of the slice: x: 2, y: 2, z: 4, core: 2. Of those that a mesh axis runs over, the one named last changes fastest.
Arguments:
- landmark_copies: float32 [8, 4, 3, 512], P('robot', 'sub'), may hold values from -6 to 6
- dual_copies: float32 [8, 4, 3, 512], P('robot', 'sub'), may hold values from -4 to 4
- visibility: int32 [8, 4, 512], P('robot', 'sub'), may hold values from 0 to 511
- block_counts: int32 [8, 4, 8], P('robot', 'sub'), may hold values from 1 to 64, as said below
- consensus_old: float32 [8, 4, 3, 512], P('robot', 'sub'), may hold values from -6 to 6
- poses: float32 [8, 4, 6, 1024], P('robot', 'sub'), may hold values from -6 to 6
- inverse_blocks: float32 [8, 4, 36, 1024], P('robot', 'sub'), may hold values from -1.8 to 1.8
- jacobians: float32 [8, 4, 18, 4096], P('robot', 'sub'), may hold values from -3 to 3
- measurements: float32 [8, 4, 3, 4096], P('robot', 'sub'), may hold values from -6 to 6
- obs_pose: int32 [8, 4, 4096], P('robot', 'sub'), may hold values from 0 to 1023
- obs_slot: int32 [8, 4, 4096], P('robot', 'sub'), may hold values from 0 to 511, as said below
- edge_to: int32 [8, 4, 1024], P('robot', 'sub'), may hold values from 0 to 4095
- edge_offset: float32 [8, 4, 6, 1024], P('robot', 'sub'), may hold values from -3 to 3
Outputs:
- refined_poses: float32 [8, 4, 6, 1024], P('robot', 'sub')
- consensus: float32 [8, 4, 3, 512], P('robot', 'sub')
- dual_new: float32 [8, 4, 3, 512], P('robot', 'sub')
- residual_norms: float32 [2], replicated
Inputs may be any that keep to these rules, and one draw needn't show every extreme that they name: block_counts[r,s,d] counts the live slots at the head of block d; for every sub index some robot receives full blocks from every robot, which robot varies with the draw. `obs_slot`: each observation names a live slot of its own device.
All inputs are finite; a program needn't handle non-finite values.
Results may differ from a plain program's by a relative error of at most 0.0001.
Values sent between devices are 32-bit elements; how exact they have to be, the bound alone decides.
No kernel may reach another device: no remote copies, remote signals or barrier semaphores. Data moves between devices by JAX's collectives and lax.ppermute only.
A program may use at most 64 MiB of HBM per device.

v0:
```python
import jax
import jax.numpy as jnp
from jax import lax
from jax.sharding import PartitionSpec as P

penalty = 2.0


def body(
    landmark_copies,
    dual_copies,
    visibility,
    block_counts,
    consensus_old,
    poses,
    inverse_blocks,
    jacobians,
    measurements,
    obs_pose,
    obs_slot,
    edge_to,
    edge_offset,
):
    copies = landmark_copies[0, 0]
    duals = dual_copies[0, 0]
    slot_ids = visibility[0]
    counts = block_counts[0, 0]
    old_estimate = consensus_old[0, 0]
    robots = lax.axis_size("robot")
    slot_count = copies.shape[1]
    block_size = slot_count // robots
    owned = old_estimate.shape[1]
    live_mask = (
        (jnp.arange(block_size)[None, :] < counts[:, None]).reshape(slot_count).astype(jnp.float32)
    )
    outgoing = jnp.concatenate([(copies + duals) * live_mask[None, :], live_mask[None, :]], axis=0)
    received, received_ids = (
        lax.all_to_all(outgoing, "robot", split_axis=1, concat_axis=1, tiled=True),
        lax.all_to_all(slot_ids, "robot", split_axis=1, concat_axis=1, tiled=True),
    )
    owner_ids = received_ids[0]
    totals = jax.vmap(lambda entries: jax.ops.segment_sum(entries, owner_ids, num_segments=owned))(
        received
    )
    consensus = (old_estimate + totals[:3]) / (1.0 + totals[3:4])
    returning = consensus[:, owner_ids]
    back = lax.all_to_all(returning, "robot", split_axis=1, concat_axis=1, tiled=True)
    differ = (copies - back) * live_mask[None, :]
    dual_new = duals + differ
    primal = jnp.sum(differ * differ)
    change = consensus - old_estimate
    dualsum = penalty * penalty * jnp.sum(totals[3:4] * change * change)
    primal_all, dual_all = lax.psum((primal, dualsum), ("robot", "sub"))
    landmark_total = owned * robots * lax.axis_size("sub")
    residual_norms = jnp.sqrt(jnp.stack([primal_all, dual_all]) / landmark_total)
    pose_block = poses[0, 0]
    pose_count = pose_block.shape[1]
    robot_all = lax.all_gather(pose_block, "sub", axis=1, tiled=True)
    pose_far = robot_all[:, edge_to[0, 0]]
    copies_at = copies[:, obs_slot[0, 0]]
    error = measurements[0, 0] - copies_at
    jac_rows = jacobians[0, 0].reshape(3, 6, error.shape[1])
    pull = jnp.sum(jac_rows * error[:, None, :], axis=0)
    pose_ids = obs_pose[0, 0]
    grad_obs = jax.vmap(
        lambda entries: jax.ops.segment_sum(entries, pose_ids, num_segments=pose_count)
    )(pull)
    grad = grad_obs + pose_far - pose_block - edge_offset[0, 0]
    inverse = inverse_blocks[0, 0].reshape(6, 6, pose_count)
    delta = jnp.sum(inverse * grad[None, :, :], axis=1)
    refined = pose_block + delta
    return (refined[None, None], consensus[None, None], dual_new[None, None], residual_norms)


def solution(mesh):
    return jax.shard_map(
        body,
        mesh=mesh,
        in_specs=(
            P("robot", "sub", None, None),
            P("robot", "sub", None, None),
            P("robot", "sub", None),
            P("robot", "sub", None),
            P("robot", "sub", None, None),
            P("robot", "sub", None, None),
            P("robot", "sub", None, None),
            P("robot", "sub", None, None),
            P("robot", "sub", None, None),
            P("robot", "sub", None),
            P("robot", "sub", None),
            P("robot", "sub", None),
            P("robot", "sub", None, None),
        ),
        out_specs=(
            P("robot", "sub", None, None),
            P("robot", "sub", None, None),
            P("robot", "sub", None, None),
            P(),
        ),
        check_vma=False,
    )
```

profile of v0, /device:TPU:0, one launch (start us, length us, event | category | flops | bytes accessed | tf_op | source)
XLA Modules:
  0.0 154.9 jit_solution(5562532823633209940)
XLA Ops:
  0.6 0.5 broadcast.115
  1.1 1.3 reduce.16
  2.5 0.7 all_to_all.22
  3.2 7.3 %all-to-all-start = ((s32[1,8,64]{2,0,1:T(1,128)}), s32[1,8,64]{2,0,1:T(1,128)S(1)}, u32[]{:S(2)}, u32[]{:S(2)}) async-start(s32[1,8,64]{2,0,1:T(1,128)} %all_to_all.22), calls=%async_computation | async-start | bytes 8192 | tf_op jit(solution)/shard_map/all_to_all | solution.py:39
  10.4 0.7 fusion.8
  11.2 0.7 fusion.9
  11.9 0.8 copy.53
  12.7 0.7 add_reduce_fusion.1
  13.5 0.1 add.79
  13.6 0.7 compare_select_fusion
  14.3 1.4 copy.52
  15.7 14.1 %gather_fusion.1 = f32[4096,3]{1,0:T(8,128)} fusion(f32[3,512]{0,1:T(8,128)S(1)} %bitcast.54, s32[4096]{0:T(1024)S(1)} %broadcast_clamp_fusion), kind=kCustom, calls=%fused_computation.1 | custom fusion | bytes 114688 | tf_op jit(solution)/shard_map/gather | solution.py:60
  29.8 3.2 %bitcast_subtract_fusion = f32[3,4096]{0,1:T(8,128)} fusion(f32[4096,3]{1,0:T(8,128)} %gather_fusion.1, f32[1,1,3,4096]{2,3,1,0:T(8,128)S(1)} %copy.52), kind=kLoop, calls=%fused_computation.5 | loop fusion | flops 12288 | bytes 147456 | tf_op jit(solution)/shard_map/sub | solution.py:61
  33.0 2.3 %copy.54 = f32[3,4096]{1,0:T(4,128)S(1)} copy(f32[3,4096]{0,1:T(8,128)} %bitcast_subtract_fusion) | data formatting | bytes 98304 | tf_op jit(solution)/shard_map/sub | solution.py:61
  35.2 0.0 copy-done.1
  35.2 0.7 reduce.1
  36.0 0.1 multiply_reduce_fusion
  36.1 2.0 %copy.55 = f32[4096,6]{1,0:T(8,128)} copy(f32[4096,6]{0,1:T(8,128)S(1)} %bitcast.57) | data formatting | bytes 196608 | tf_op jit(solution)/shard_map/reduce_sum | solution.py:63
  38.1 0.2 copy.51
  38.3 15.8 %all-gather = f32[1,1,6,4096]{2,3,1,0:T(8,128)S(1)} all-gather(f32[1,1,6,1024]{2,3,1,0:T(8,128)S(1)} %copy.51), channel_id=2, replica_groups=mesh['robot'=8,'sub'=4] {'sub'}, dimensions={3}, use_global_device_ids=true | all-gather | bytes 122880 | tf_op jit(solution)/shard_map/all_gather | solution.py:58
  54.1 1.0 copy.57
  55.1 2.8 %gather_fusion = f32[1024,6]{1,0:T(8,128)S(1)} fusion(f32[6,4096]{0,1:T(8,128)S(1)} %bitcast.55, s32[1024]{0:T(1024)S(1)} %broadcast_clamp_fusion.1), kind=kCustom, calls=%fused_computation | custom fusion | bytes 53248 | tf_op jit(solution)/shard_map/gather | solution.py:59
  58.0 0.0 copy-start.2
  58.0 22.9 %scatter_fusion = f32[6,1024]{0,1:T(8,128)S(1)} fusion(f32[6,1024]{0,1:T(8,128)S(1)} %bitcast.53, s32[4096]{0:T(1024)S(1)} %bitcast.67, f32[4096,6]{1,0:T(8,128)} %copy.55), kind=kCustom, calls=%fused_computation.3 | custom fusion | flops 24576 | bytes 311296 | tf_op jit(solution)/shard_map/vmap()/scatter-add | solution.py:66
  80.9 0.0 copy-done
  80.9 0.0 copy-start.8
  80.9 0.1 bitcast_subtract_fusion.1
  81.0 0.2 copy.58
  81.2 0.4 reduce
  81.6 0.0 copy-start.4
  81.6 0.0 copy-start.6
  81.6 0.1 multiply_reduce_fusion.1
  81.7 0.7 reshape.262
  82.4 0.1 copy.59
  82.6 0.0 all-to-all-done
  82.6 6.0 %all-to-all-start.1 = ((f32[8,1,256]{2,1,0:T(1,128)}), f32[8,1,256]{2,1,0:T(1,128)S(1)}, u32[]{:S(2)}, u32[]{:S(2)}) async-start(f32[8,1,256]{2,1,0:T(1,128)} %reshape.262), calls=%async_computation.1 | async-start | bytes 16384 | tf_op jit(solution)/shard_map/all_to_all | solution.py:38
  88.6 0.1 broadcast_in_dim_squeeze.8
  88.7 0.7 reduce.17
  89.3 0.1 reshape.227
  89.4 5.7 %all-to-all-done.1 = f32[8,1,256]{2,1,0:T(1,128)S(1)} async-done(((f32[8,1,256]{2,1,0:T(1,128)}), f32[8,1,256]{2,1,0:T(1,128)S(1)}, u32[]{:S(2)}, u32[]{:S(2)}) %all-to-all-start.1) | async-done | bytes 8224 | tf_op jit(solution)/shard_map/all_to_all | solution.py:38
  95.1 0.5 broadcast.117
  95.6 0.7 reduce.18
  96.3 0.1 reshape.263
  96.4 0.1 reshape.226
  96.5 0.1 copy.62
  96.6 2.3 %scatter_custom_fusion.1 = f32[4,512]{0,1:T(8,128)S(1)} fusion(s32[512]{0:T(512)S(1)} %reshape.227, f32[512,4]{1,0:T(8,128)S(1)} %copy.62, f32[]{:T(128)} %constant.10.clone.1), kind=kCustom, calls=%fused_computation.21 | custom fusion | flops 2048 | bytes 8196 | tf_op jit(solution)/shard_map/vmap()/scatter-add | solution.py:42
  98.9 0.3 slice_reduce_fusion
  99.2 0.8 fusion
  100.0 1.0 gather_fusion.2
  101.1 0.1 copy.63
  101.2 0.7 reshape.264
  101.9 3.3 %all-to-all-start.2 = ((f32[8,1,192]{2,1,0:T(1,128)}), f32[8,1,192]{2,1,0:T(1,128)S(1)}, u32[]{:S(2)}, u32[]{:S(2)}) async-start(f32[8,1,192]{2,1,0:T(1,128)} %reshape.264), calls=%async_computation.2 | async-start | bytes 16384 | tf_op jit(solution)/shard_map/all_to_all | solution.py:47
  105.3 0.6 reshape_add_fusion
  105.9 0.1 reshape.192
  106.0 0.7 copy.68
  107.3 4.4 %all-to-all-done.2 = f32[8,1,192]{2,1,0:T(1,128)S(1)} async-done(((f32[8,1,192]{2,1,0:T(1,128)}), f32[8,1,192]{2,1,0:T(1,128)S(1)}, u32[]{:S(2)}, u32[]{:S(2)}) %all-to-all-start.2) | async-done | bytes 6176 | tf_op jit(solution)/shard_map/all_to_all | solution.py:47
  111.7 0.7 reduce.19
  112.4 0.1 reshape.265
  112.5 0.2 copy.67
  112.6 0.1 all_to_all.28
  112.7 0.7 fusion.4
  113.5 0.6 copy.69
  114.1 38.9 %all-reduce = (f32[1]{0:T(128)}, f32[1]{0:T(128)}) all-reduce(f32[1]{0:T(128)} %bitcast.22, f32[1]{0:T(128)} %bitcast.21), channel_id=1, replica_groups=mesh['robot'=8,'sub'=4] {'robot','sub'}, use_global_device_ids=true, to_apply=%region_7.0 | all-reduce | flops 2 | bytes 16 | tf_op jit(solution)/shard_map/psum | solution.py:53
  153.0 1.9 %fusion.10 = f32[2]{0:T(128)} fusion(f32[1]{0:T(128)} %get-tuple-element.22, f32[1]{0:T(128)} %get-tuple-element.23), kind=kLoop, calls=%fused_computation.41 | loop fusion | flops 4 | bytes 16 | tf_op jit(solution)/shard_map/sqrt | solution.py:55
  (27 shorter events, 0.2 us)
Async XLA Ops:
  3.2 79.4 %all-to-all-start = ((s32[1,8,64]{2,0,1:T(1,128)}), s32[1,8,64]{2,0,1:T(1,128)S(1)}, u32[]{:S(2)}, u32[]{:S(2)}) async-start(s32[1,8,64]{2,0,1:T(1,128)} %all_to_all.22), calls=%async_computation | async-start | bytes 8192 | tf_op jit(solution)/shard_map/all_to_all | solution.py:39
  33.0 2.3 %copy-start.1 = (f32[1,1,18,4096]{3,1,2,0:T(1,128)S(1)}, f32[1,1,18,4096]{3,1,2,0:T(1,128)}, u32[]{:S(2)}) copy-start(f32[1,1,18,4096]{3,1,2,0:T(1,128)} %param.20) | copy-start | bytes 884740
  35.2 2.8 %copy-start.3 = (f32[1,1,6,1024]{3,1,2,0:T(1,128)S(1)}, f32[1,1,6,1024]{3,1,2,0:T(1,128)}, u32[]{:S(2)}) copy-start(f32[1,1,6,1024]{3,1,2,0:T(1,128)} %param.18) | copy-start | bytes 73732
  38.1 16.0 %copy-start.9 = (s32[1,1,1024]{2,1,0:T(1,128)S(1)}, s32[1,1,1024]{2,1,0:T(1,128)}, u32[]{:S(2)}) copy-start(s32[1,1,1024]{2,1,0:T(1,128)} %param.24) | copy-start | bytes 12292
  38.1 16.0 %copy-start.5 = (f32[1,1,6,1024]{3,1,2,0:T(1,128)S(1)}, f32[1,1,6,1024]{3,1,2,0:T(1,128)}, u32[]{:S(2)}) copy-start(f32[1,1,6,1024]{3,1,2,0:T(1,128)} %param.25) | copy-start | bytes 73732
  38.1 19.9 %copy-start.7 = (s32[1,1,4096]{2,1,0:T(1,128)S(1)}, s32[1,1,4096]{2,1,0:T(1,128)}, u32[]{:S(2)}) copy-start(s32[1,1,4096]{2,1,0:T(1,128)} %param.22) | copy-start | bytes 49156
  57.9 23.0 %copy-start = (f32[1,1,6,1024]{2,3,1,0:T(8,128)S(1)}, f32[1,1,6,1024]{2,3,1,0:T(8,128)}, u32[]{:S(2)}) copy-start(f32[1,1,6,1024]{2,3,1,0:T(8,128)} %copy.57) | copy-start | bytes 73732
  58.0 23.2 %copy-start.2 = (f32[1,1,36,1024]{3,1,2,0:T(1,128)S(1)}, f32[1,1,36,1024]{3,1,2,0:T(1,128)}, u32[]{:S(2)}) copy-start(f32[1,1,36,1024]{3,1,2,0:T(1,128)} %param.19) | copy-start | bytes 442372
  80.9 1.5 copy-start.8
  81.6 31.9 %copy-start.4 = (f32[1,1,3,512]{3,1,2,0:T(1,128)S(1)}, f32[1,1,3,512]{3,1,2,0:T(1,128)}, u32[]{:S(2)}) copy-start(f32[1,1,3,512]{3,1,2,0:T(1,128)} %param.13) | copy-start | bytes 18436
  81.6 31.9 %copy-start.6 = (f32[1,1,3,512]{3,1,2,0:T(1,128)S(1)}, f32[1,1,3,512]{3,1,2,0:T(1,128)}, u32[]{:S(2)}) copy-start(f32[1,1,3,512]{3,1,2,0:T(1,128)} %param.14) | copy-start | bytes 18436
  82.6 12.5 %all-to-all-start.1 = ((f32[8,1,256]{2,1,0:T(1,128)}), f32[8,1,256]{2,1,0:T(1,128)S(1)}, u32[]{:S(2)}, u32[]{:S(2)}) async-start(f32[8,1,256]{2,1,0:T(1,128)} %reshape.262), calls=%async_computation.1 | async-start | bytes 16384 | tf_op jit(solution)/shard_map/all_to_all | solution.py:38
  101.9 9.8 %all-to-all-start.2 = ((f32[8,1,192]{2,1,0:T(1,128)}), f32[8,1,192]{2,1,0:T(1,128)S(1)}, u32[]{:S(2)}, u32[]{:S(2)}) async-start(f32[8,1,192]{2,1,0:T(1,128)} %reshape.264), calls=%async_computation.2 | async-start | bytes 16384 | tf_op jit(solution)/shard_map/all_to_all | solution.py:47
where the time goes:
time: 156 us; the launch traced here: 155 us
  blocking collectives  54.7 us (35%)
  other arithmetic  40.4 us (26%)
  local copies, waits for them, and re-layouts  31.6 us (20%)
  starting transfers between devices  16.6 us (11%)
  waiting for transfers between devices  10.1 us (6%)
  between operations  1.6 us (1%)
    psum x1, blocking collectives, body(): primal_all, dual_all = lax.psum((primal, dualsum), ('robot', 'sub'))  38.9 us
    scatter-add x1, other arithmetic, body(): jax.ops.segment_sum(entries, pose_ids, num_segments=pose_count)  22.9 us
    all_gather x1, blocking collectives, body(): robot_all = lax.all_gather(pose_block, 'sub', axis=1, tiled=True)  15.8 us
    gather x1, local copies, waits for them, and re-layouts, body(): copies_at = copies[:, obs_slot[0, 0]]  14.1 us
    all_to_all x1, starting transfers between devices, body(): lax.all_to_all(slot_ids, 'robot', split_axis=1, concat_axis=1, tiled=True)  7.28 us
    unnamed x32, local copies, waits for them, and re-layouts  7.06 us
    all_to_all x1, starting transfers between devices, body(): lax.all_to_all(outgoing, 'robot', split_axis=1, concat_axis=1, tiled=True)  6.01 us
    all_to_all x1, waiting for transfers between devices, body(): lax.all_to_all(outgoing, 'robot', split_axis=1, concat_axis=1, tiled=True)  5.69 us
  transfers between devices with their start and end apart: 3, of which 2 were waited for; matrix products, arithmetic and copies ran while one was open for 38% of the time, Pallas kernels for 0%

commit v1 on v0

--- a/solution.py
+++ b/solution.py
@@ -55,7 +55,14 @@
     residual_norms = jnp.sqrt(jnp.stack([primal_all, dual_all]) / landmark_total)
     pose_block = poses[0, 0]
     pose_count = pose_block.shape[1]
-    robot_all = lax.all_gather(pose_block, "sub", axis=1, tiled=True)
+    size = lax.axis_size("sub")
+    right = [(i, (i + 1) % size) for i in range(size)]
+    shards = [pose_block]
+    for far in range(1, size):
+        shards = [lax.ppermute(shards[0], "sub", right), *shards]
+    whole = jnp.concatenate(shards, axis=1)
+    places = (lax.axis_index("sub") + 1) * shards[-1].shape[1]
+    robot_all = jnp.roll(whole, places, axis=1)
     pose_far = robot_all[:, edge_to[0, 0]]
     copies_at = copies[:, obs_slot[0, 0]]
     error = measurements[0, 0] - copies_at

time: 156 us -> 148 us (0.949)
  blocking collectives: 54.7 us -> 40.7 us
  waiting for transfers between devices: 10.1 us -> 12.6 us
  other arithmetic: 40.4 us -> 42.4 us
    all_gather x1 -> x0, blocking collectives: 15.8 us -> none  [body(): robot_all = lax.all_gather(pose_block, 'sub', axis=1, tiled=True)]
    ppermute x0 -> x3, waiting for transfers between devices: none -> 6.12 us  [body(): shards = [lax.ppermute(shards[0], 'sub', right), *shards]]
    all_to_all x1, waiting for transfers between devices: 4.39 us -> 0.81 us  [body(): lax.all_to_all(returning, 'robot', split_axis=1, concat_axis=1, tiled=True)]
    unnamed x32 -> x35, local copies, waits for them, and re-layouts: 7.06 us -> 9.34 us
    psum x1, blocking collectives: 38.9 us -> 40.7 us  [body(): primal_all, dual_all = lax.psum((primal, dualsum), ('robot', 'sub'))]
    sub x1, local copies, waits for them, and re-layouts: 2.25 us -> 0.62 us  [body(): error = measurements[0, 0] - copies_at]
  transfers between devices with their start and end apart: 3 -> 6, of which waited for: 2 -> 3; matrix products, arithmetic and copies ran while one was open for 38% -> 31% of each run, Pallas kernels for 0% -> 0%
where the time goes in v1:
time: 148 us; the launch traced here: 147 us
  other arithmetic  42.4 us (29%)
  blocking collectives  40.7 us (28%)
  local copies, waits for them, and re-layouts  33.1 us (22%)
  starting transfers between devices  16.8 us (11%)
  waiting for transfers between devices  12.6 us (9%)
  between operations  1.65 us (1%)
    psum x1, blocking collectives, body(): primal_all, dual_all = lax.psum((primal, dualsum), ('robot', 'sub'))  40.7 us
    scatter-add x1, other arithmetic, body(): jax.ops.segment_sum(entries, pose_ids, num_segments=pose_count)  22.9 us
    gather x1, local copies, waits for them, and re-layouts, body(): copies_at = copies[:, obs_slot[0, 0]]  14.1 us
    unnamed x35, local copies, waits for them, and re-layouts  9.34 us
    all_to_all x1, starting transfers between devices, body(): lax.all_to_all(slot_ids, 'robot', split_axis=1, concat_axis=1, tiled=True)  6.8 us
    ppermute x3, waiting for transfers between devices, body(): shards = [lax.ppermute(shards[0], 'sub', right), *shards]  6.12 us
    all_to_all x1, starting transfers between devices, body(): lax.all_to_all(outgoing, 'robot', split_axis=1, concat_axis=1, tiled=True)  6.01 us
    all_to_all x1, waiting for transfers between devices, body(): lax.all_to_all(outgoing, 'robot', split_axis=1, concat_axis=1, tiled=True)  5.69 us
  transfers between devices with their start and end apart: 6, of which 3 were waited for; matrix products, arithmetic and copies ran while one was open for 31% of the time, Pallas kernels for 0%

profile of v1, /device:TPU:0, one launch (start us, length us, event | category | flops | bytes accessed | tf_op | source)
XLA Modules:
  0.0 147.2 jit_solution(2346915817919433879)
XLA Ops:
  0.6 1.0 copy.84
  1.6 0.5 collective-permute-start
  2.1 0.5 broadcast.116
  2.6 1.3 reduce.16
  4.0 0.7 all_to_all.22
  4.7 6.8 %all-to-all-start = ((s32[1,8,64]{2,0,1:T(1,128)}), s32[1,8,64]{2,0,1:T(1,128)S(1)}, u32[]{:S(2)}, u32[]{:S(2)}) async-start(s32[1,8,64]{2,0,1:T(1,128)} %all_to_all.22), calls=%async_computation | async-start | bytes 8192 | tf_op jit(solution)/shard_map/all_to_all | solution.py:39
  11.5 0.7 fusion.8
  12.2 0.7 fusion.9
  12.9 0.7 compare_select_fusion.1
  13.6 0.8 copy.86
  14.5 0.7 compare_select_fusion
  15.2 2.7 %copy.85 = f32[1,1,3,4096]{2,3,1,0:T(8,128)} copy(f32[1,1,3,4096]{3,1,2,0:T(1,128)} %param.21) | data formatting | bytes 98304 | tf_op args[8]
  17.9 0.7 add_reduce_fusion.1
  18.7 0.1 add.95
  18.8 14.1 %gather_fusion.1 = f32[4096,3]{1,0:T(8,128)} fusion(f32[3,512]{0,1:T(8,128)S(1)} %bitcast.54, s32[4096]{0:T(1024)S(1)} %broadcast_clamp_fusion), kind=kCustom, calls=%fused_computation.1 | custom fusion | bytes 114688 | tf_op jit(solution)/shard_map/gather | solution.py:67
  32.8 2.4 %bitcast_subtract_fusion = f32[3,4096]{0,1:T(8,128)S(1)} fusion(f32[4096,3]{1,0:T(8,128)} %gather_fusion.1, f32[1,1,3,4096]{2,3,1,0:T(8,128)} %copy.85), kind=kLoop, calls=%fused_computation.5 | loop fusion | flops 12288 | bytes 147456 | tf_op jit(solution)/shard_map/sub | solution.py:68
  35.3 0.0 copy-start.4
  35.3 0.6 copy.87
  36.0 1.7 %reduce.1 = f32[18,4096]{1,0:T(8,128)S(1)} reduce(f32[1,1,18,4096]{3,1,2,0:T(1,128)} %param.20, f32[]{:T(128)} %constant.61), dimensions={0,1}, to_apply=%param.20.reduce_sub_computation | reduce | bytes 589828 | tf_op args[7]
  37.8 0.7 reshape.261
  38.5 0.1 copy.91
  38.6 6.0 %all-to-all-start.1 = ((f32[8,1,256]{2,1,0:T(1,128)}), f32[8,1,256]{2,1,0:T(1,128)S(1)}, u32[]{:S(2)}, u32[]{:S(2)}) async-start(f32[8,1,256]{2,1,0:T(1,128)} %reshape.261), calls=%async_computation.1 | async-start | bytes 16384 | tf_op jit(solution)/shard_map/all_to_all | solution.py:38
  44.6 0.1 broadcast_in_dim_squeeze.8
  44.7 0.7 reduce.17
  45.4 0.1 reshape.227
  45.5 5.7 %all-to-all-done.1 = f32[8,1,256]{2,1,0:T(1,128)S(1)} async-done(((f32[8,1,256]{2,1,0:T(1,128)}), f32[8,1,256]{2,1,0:T(1,128)S(1)}, u32[]{:S(2)}, u32[]{:S(2)}) %all-to-all-start.1) | async-done | bytes 8224 | tf_op jit(solution)/shard_map/all_to_all | solution.py:38
  51.2 0.5 broadcast.118
  51.7 0.7 reduce.18
  52.3 0.1 reshape.262
  52.4 0.1 reshape.226
  52.5 0.1 copy.94
  52.7 2.3 %scatter_custom_fusion.1 = f32[4,512]{0,1:T(8,128)S(1)} fusion(s32[512]{0:T(512)S(1)} %reshape.227, f32[512,4]{1,0:T(8,128)S(1)} %copy.94, f32[]{:T(128)} %constant.44.clone.1), kind=kCustom, calls=%fused_computation.20 | custom fusion | flops 2048 | bytes 8196 | tf_op jit(solution)/shard_map/vmap()/scatter-add | solution.py:42
  55.0 0.3 slice_reduce_fusion
  55.3 0.8 fusion
  56.1 1.0 gather_fusion.2
  57.1 0.1 copy.95
  57.3 0.7 reshape.263
  58.0 3.3 %all-to-all-start.2 = ((f32[8,1,192]{2,1,0:T(1,128)}), f32[8,1,192]{2,1,0:T(1,128)S(1)}, u32[]{:S(2)}, u32[]{:S(2)}) async-start(f32[8,1,192]{2,1,0:T(1,128)} %reshape.263), calls=%async_computation.2 | async-start | bytes 16384 | tf_op jit(solution)/shard_map/all_to_all | solution.py:47
  61.3 0.1 multiply_reduce_fusion
  61.4 0.1 reshape.192
  61.5 2.0 %copy.88 = f32[4096,6]{1,0:T(8,128)} copy(f32[4096,6]{0,1:T(8,128)S(1)} %bitcast.56) | data formatting | bytes 196608 | tf_op jit(solution)/shard_map/reduce_sum | solution.py:70
  63.5 1.0 copy.89
  64.5 0.3 reduce
  64.8 0.7 reshape_squeeze.6
  65.5 0.7 copy.100
  66.9 0.1 collective-permute-start.1
  67.0 0.8 all-to-all-done.2
  67.8 0.7 reduce.19
  68.5 0.1 reshape.264
  68.5 0.2 copy.99
  68.7 0.1 all_to_all.28
  68.8 0.7 fusion.4
  69.5 40.7 %all-reduce = (f32[1]{0:T(128)}, f32[1]{0:T(128)}) all-reduce(f32[1]{0:T(128)} %bitcast.21, f32[1]{0:T(128)} %bitcast.20), channel_id=1, replica_groups=mesh['robot'=8,'sub'=4] {'robot','sub'}, use_global_device_ids=true, to_apply=%region_7.8 | all-reduce | flops 2 | bytes 16 | tf_op jit(solution)/shard_map/psum | solution.py:53
  110.3 1.9 %fusion.10 = f32[2]{0:T(128)} fusion(f32[1]{0:T(128)} %get-tuple-element.26, f32[1]{0:T(128)} %get-tuple-element.27), kind=kLoop, calls=%fused_computation.48 | loop fusion | flops 4 | bytes 16 | tf_op jit(solution)/shard_map/sqrt | solution.py:55
  112.2 0.6 copy.101
  112.8 6.1 %collective-permute-done.2 = f32[6,1024]{0,1:T(8,128)S(1)} collective-permute-done((f32[6,1024]{0,1:T(8,128)S(1)}, f32[6,1024]{0,1:T(8,128)S(1)}, u32[]{:S(2)}, u32[]{:S(2)}) %collective-permute-start.2) | collective-permute-done | bytes 24608 | tf_op jit(solution)/shard_map/ppermute | solution.py:62
  119.1 0.0 copy-start.6
  119.3 0.1 constant_dynamic-slice_fusion
  119.4 2.8 %gather_fusion = f32[1024,6]{1,0:T(8,128)S(1)} fusion(f32[6,4096]{0,1:T(8,128)S(1)} %constant_dynamic-slice_fusion, s32[1024]{0:T(1024)S(1)} %get-tuple-element.31), kind=kCustom, calls=%fused_computation | custom fusion | bytes 53248 | tf_op jit(solution)/shard_map/gather | solution.py:66
  122.2 22.9 %scatter_fusion = f32[6,1024]{0,1:T(8,128)S(1)} fusion(f32[6,1024]{0,1:T(8,128)S(1)} %bitcast.53, s32[4096]{0:T(1024)S(1)} %bitcast.66, f32[4096,6]{1,0:T(8,128)} %copy.88), kind=kCustom, calls=%fused_computation.3 | custom fusion | flops 24576 | bytes 311296 | tf_op jit(solution)/shard_map/vmap()/scatter-add | solution.py:73
  145.1 1.1 bitcast_subtract_fusion.1
  146.3 0.2 copy.90
  146.4 0.1 multiply_reduce_fusion.1
  146.5 0.6 reshape_add_fusion
  (36 shorter events, 0.4 us)
Async XLA Ops:
  1.6 65.3 %collective-permute-start = (f32[6,1024]{0,1:T(8,128)S(1)}, f32[6,1024]{0,1:T(8,128)S(1)}, u32[]{:S(2)}, u32[]{:S(2)}) collective-permute-start(f32[6,1024]{0,1:T(8,128)S(1)} %bitcast.52), channel_id=1, source_target_pairs={{0,1},{1,2},{2,3},{3,0},{4,5},{5,6},{6,7},{7,4},{8,9},{9,10},{10,1... | collective-permute-start | bytes 73736 | tf_op jit(solution)/shard_map/ppermute | solution.py:62
  4.7 33.9 %all-to-all-start = ((s32[1,8,64]{2,0,1:T(1,128)}), s32[1,8,64]{2,0,1:T(1,128)S(1)}, u32[]{:S(2)}, u32[]{:S(2)}) async-start(s32[1,8,64]{2,0,1:T(1,128)} %all_to_all.22), calls=%async_computation | async-start | bytes 8192 | tf_op jit(solution)/shard_map/all_to_all | solution.py:39
  32.8 5.6 %copy-start.7 = (f32[1,1,3,512]{3,1,2,0:T(1,128)S(1)}, f32[1,1,3,512]{3,1,2,0:T(1,128)}, u32[]{:S(2)}) copy-start(f32[1,1,3,512]{3,1,2,0:T(1,128)} %param.17) | copy-start | bytes 18436
  35.3 28.1 %copy-start.4 = (f32[1,1,6,1024]{3,1,2,0:T(1,128)S(1)}, f32[1,1,6,1024]{3,1,2,0:T(1,128)}, u32[]{:S(2)}) copy-start(f32[1,1,6,1024]{3,1,2,0:T(1,128)} %param.25) | copy-start | bytes 73732
  35.9 28.5 %copy-start.1 = (f32[1,1,36,1024]{3,1,2,0:T(1,128)S(1)}, f32[1,1,36,1024]{3,1,2,0:T(1,128)}, u32[]{:S(2)}) copy-start(f32[1,1,36,1024]{3,1,2,0:T(1,128)} %param.19) | copy-start | bytes 442372
  35.9 32.8 %copy-start.3 = (f32[1,1,3,512]{3,1,2,0:T(1,128)S(1)}, f32[1,1,3,512]{3,1,2,0:T(1,128)}, u32[]{:S(2)}) copy-start(f32[1,1,3,512]{3,1,2,0:T(1,128)} %param.13) | copy-start | bytes 18436
  36.0 32.8 %copy-start.5 = (f32[1,1,3,512]{3,1,2,0:T(1,128)S(1)}, f32[1,1,3,512]{3,1,2,0:T(1,128)}, u32[]{:S(2)}) copy-start(f32[1,1,3,512]{3,1,2,0:T(1,128)} %param.14) | copy-start | bytes 18436
  38.6 12.5 %all-to-all-start.1 = ((f32[8,1,256]{2,1,0:T(1,128)}), f32[8,1,256]{2,1,0:T(1,128)S(1)}, u32[]{:S(2)}, u32[]{:S(2)}) async-start(f32[8,1,256]{2,1,0:T(1,128)} %reshape.261), calls=%async_computation.1 | async-start | bytes 16384 | tf_op jit(solution)/shard_map/all_to_all | solution.py:38
  58.0 9.8 %all-to-all-start.2 = ((f32[8,1,192]{2,1,0:T(1,128)}), f32[8,1,192]{2,1,0:T(1,128)S(1)}, u32[]{:S(2)}, u32[]{:S(2)}) async-start(f32[8,1,192]{2,1,0:T(1,128)} %reshape.263), calls=%async_computation.2 | async-start | bytes 16384 | tf_op jit(solution)/shard_map/all_to_all | solution.py:47
  66.9 43.4 %collective-permute-start.1 = (f32[6,1024]{0,1:T(8,128)S(1)}, f32[6,1024]{0,1:T(8,128)S(1)}, u32[]{:S(2)}, u32[]{:S(2)}) collective-permute-start(f32[6,1024]{0,1:T(8,128)S(1)} %collective-permute-done), channel_id=1, source_target_pairs={{0,1},{1,2},{2,3},{3,0},{4,5},{5,6},{6,7},{7,4},{8,9},{9,10},{10,1... | collective-permute-start | bytes 73736 | tf_op jit(solution)/shard_map/ppermute | solution.py:62
  110.3 8.6 %collective-permute-start.2 = (f32[6,1024]{0,1:T(8,128)S(1)}, f32[6,1024]{0,1:T(8,128)S(1)}, u32[]{:S(2)}, u32[]{:S(2)}) collective-permute-start(f32[6,1024]{0,1:T(8,128)S(1)} %collective-permute-done.1), channel_id=1, source_target_pairs={{0,1},{1,2},{2,3},{3,0},{4,5},{5,6},{6,7},{7,4},{8,9},{9,10},{10,1... | collective-permute-start | bytes 73736 | tf_op jit(solution)/shard_map/ppermute | solution.py:62
  119.1 3.2 %copy-start.6 = (s32[1,1,4096]{2,1,0:T(1,128)S(1)}, s32[1,1,4096]{2,1,0:T(1,128)}, u32[]{:S(2)}) copy-start(s32[1,1,4096]{2,1,0:T(1,128)} %param.22) | copy-start | bytes 49156
  119.2 27.2 %copy-start = (f32[6,6,1024]{2,1,0:T(8,128)S(1)}, f32[6,6,1024]{2,1,0:T(8,128)}, u32[]{:S(2)}) copy-start(f32[6,6,1024]{2,1,0:T(8,128)} %reshape_squeeze.6) | copy-start | bytes 442372
  119.3 27.3 %copy-start.2 = (f32[1,1,6,1024]{3,1,2,0:T(1,128)S(1)}, f32[1,1,6,1024]{3,1,2,0:T(1,128)}, u32[]{:S(2)}) copy-start(f32[1,1,6,1024]{3,1,2,0:T(1,128)} %param.18) | copy-start | bytes 73732
